TPU v7x, 32 devices: a whole 2x2x4 slice. The times are simulated.
32 devices in a mesh: band: 8 (over z, x), patch: 4 (over y, core).
Axes of the slice: x: 2, y: 2, z: 4, core: 2. Of those that a mesh axis runs over, the one named last changes fastest.
Arguments:
- latents: bfloat16 [8, 10240, 512], P('band', 'patch'), may hold values from -6 to 6
- owners: int32 [16], replicated, may hold values from 0 to 3, as said below
- block_rows: int32 [16, 128], replicated, may hold values from 0 to 2559
- interp_weights: bfloat16 [16, 1024, 128], P('band', 'patch'), may hold values from -0.5 to 0.5
- w_first: bfloat16 [8, 512, 512], P('band'), may hold values from -0.25 to 0.25
- b_first: float32 [8, 512], P('band'), may hold values from -3 to 3
- w_second: bfloat16 [8, 512, 512], P('band'), may hold values from -0.25 to 0.25
- b_second: float32 [8, 512], P('band'), may hold values from -4 to 4
- gain: float32 [8, 512], P('band'), may hold values from 0.1 to 1.9
- w_out: bfloat16 [8, 12, 512], P('band'), may hold values from -0.25 to 0.25
- b_out: float32 [8, 12], P('band'), may hold values from -4 to 4
Outputs:
- grid_fields: float32 [8, 12, 16384], P('band', None, 'patch')
Inputs may be any that keep to these rules, and one draw needn't show every extreme that they name: `owners`: no patch owns more than 8 tiles, and one patch owns exactly 8.
All inputs are finite; a program needn't handle non-finite values.
Results may differ from a plain program's by a relative error of at most 0.003.
Values may be sent and summed in bfloat16 or wider, within the bound.
A program may use at most 64 MiB of HBM per device.

v0:
```python
import jax
import jax.numpy as jnp
from jax import lax
from jax.sharding import PartitionSpec as P


def decode_rows(interp, w_first, b_first, w_second, b_second, gain, w_out, b_out):
    hidden = jax.nn.silu(
        jnp.dot(interp, w_first, preferred_element_type=jnp.float32) + b_first
    ).astype(jnp.bfloat16)
    second = jnp.dot(hidden, w_second, preferred_element_type=jnp.float32) + b_second
    mean_value = jnp.mean(second, axis=-1, keepdims=True)
    centred = second - mean_value
    variance = jnp.mean(centred * centred, axis=-1, keepdims=True)
    normed = (centred * lax.rsqrt(variance + 1e-05) * gain).astype(jnp.bfloat16)
    result = lax.dot_general(
        w_out, normed, (((1,), (1,)), ((), ())), preferred_element_type=jnp.float32
    )
    return result + b_out[:, None]


def body(
    latents,
    owners,
    block_rows,
    interp_weights,
    w_first,
    b_first,
    w_second,
    b_second,
    gain,
    w_out,
    b_out,
):
    tile_count = owners.shape[0]
    cell_count = interp_weights.shape[1]
    channels = w_out.shape[1]
    local_latents = latents[0]
    width = local_latents.shape[1]
    weights_all = lax.all_gather(interp_weights, "band", axis=0, tiled=True)

    def decode_tile(tile_index, block):
        tile_weights = lax.dynamic_index_in_dim(weights_all, tile_index, 0, keepdims=False)
        interp = jnp.dot(tile_weights, block, preferred_element_type=jnp.float32).astype(
            jnp.bfloat16
        )
        return decode_rows(
            interp, w_first[0], b_first[0], w_second[0], b_second[0], gain[0], w_out[0], b_out[0]
        )

    empty = jnp.zeros((channels, tile_count, cell_count), jnp.float32)
    my_index = lax.axis_index("patch")
    own_tiles = jnp.take(local_latents, block_rows.reshape(-1), axis=0).reshape(
        tile_count, -1, width
    )
    mine = (owners == my_index)[:, None, None]
    filled = jnp.where(mine, own_tiles.astype(jnp.float32), jnp.float32(0.0))
    all_blocks = lax.psum(filled.astype(jnp.bfloat16), "patch")

    def visit_summed(turn_index, buffer):
        tile_index = turn_index % tile_count
        block = lax.dynamic_index_in_dim(all_blocks, tile_index, 0, keepdims=False)
        result = decode_tile(tile_index, block)
        return lax.dynamic_update_index_in_dim(buffer, result, tile_index, 1)

    decoded = lax.fori_loop(0, tile_count, visit_summed, empty)
    regrid = lax.all_to_all(decoded, "patch", split_axis=1, concat_axis=2, tiled=True)
    return regrid.reshape(channels, -1)[None]


def solution(mesh):
    return jax.shard_map(
        body,
        mesh=mesh,
        in_specs=(
            P("band", "patch", None),
            P(),
            P(),
            P("band", "patch", None),
            P("band", None, None),
            P("band", None),
            P("band", None, None),
            P("band", None),
            P("band", None),
            P("band", None, None),
            P("band", None),
        ),
        out_specs=P("band", None, "patch"),
        check_vma=False,
    )
```

profile of v0, /device:TPU:24, one launch (start us, length us, event | category | flops | bytes accessed | tf_op | source)
XLA Modules:
  0.0 142.6 jit_solution(14935995324864705536)
XLA Ops:
  7.4 0.9 compare_and_fusion
  8.2 0.7 compare_select_fusion
  9.1 9.2 %gather_fusion = bf16[2048,512]{1,0:T(8,128)(2,1)} fusion(bf16[2560,512]{1,0:T(8,128)(2,1)S(1)} %bitcast.62, s32[2048]{0:T(1024)S(1)} %broadcast_clamp_fusion), kind=kCustom, calls=%fused_computation | custom fusion | bytes 4202496 | tf_op jit(solution)/shard_map/jit(_take)/gather | solution.py:53
  18.3 2.9 %select_convert_fusion = bf16[16,128,512]{2,1,0:T(8,128)(2,1)} fusion(bf16[16,128,512]{2,1,0:T(8,128)(2,1)} %bitcast.63, pred[16]{0:T(512)(128)(4,1)S(1)} %broadcast_compare_fusion, pred[16,128]{1,0:T(8,128)(4,1)S(1)} %compare_and_fusion), kind=kLoop, calls=%fused_computation.23 | loop fusion | flops 4194304 | bytes 4196368 | tf_op jit(solution)/shard_map/convert_element_type | solution.py:58
  21.3 0.5 all-gather.2.cloned.1.call-update
  21.9 51.9 %all-reduce.2.cloned.1.call-done = bf16[16,128,512]{2,1,0:T(8,128)(2,1)} async-done(((bf16[16,128,512]{2,1,0:T(8,128)(2,1)}), bf16[16,128,512]{2,1,0:T(8,128)(2,1)}) %all-reduce.2.cloned.1.call-update) | async-done | bytes 2097168 | tf_op jit(solution)/shard_map/psum | solution.py:58
  73.8 0.7 broadcast_in_dim.43
  74.6 50.2 %while.15 = (s32[]{:T(128)}, f32[12,16,256]{2,0,1:T(8,128)}, bf16[16,256,128]{2,1,0:T(8,128)(2,1)}, bf16[16,128,512]{2,1,0:T(8,128)(2,1)}, bf16[1,512,512]{2,1,0...) while((s32[]{:T(128)}, f32[12,16,256]{2,0,1:T(8,128)}, ...), condition=%wide.region_4.5_spmd, body=%wide.region_1.4_spmd.sunk | while | flops 307236096 | bytes 3387677 | solution.py:66
  74.6 1.7 %multiply_convert_fusion.6 = bf16[256,512]{1,0:T(8,128)(2,1)S(1)} fusion(bf16[1,512,512]{2,1,0:T(8,128)(2,1)} %get-tuple-element.400, f32[512]{0:T(512)S(1)} %bitcast.71, bf16[16,128,512]{2,1,0:T(8,128)(2,1)} %get-tuple-element.399, s32[]{:T(128)S(6)} %select_n.74, bf16[16,256,128]{2,1,0:T(8,128)(2,1)} %get-tuple-element.398), kind=kOutput, calls=%fused_computation.11.clone.1 | convolution fusion | flops 168689664 | bytes 986112 | tf_op jit(solution)/shard_map/while/body/eval_jaxpr/dot_general | solution.py:9
  76.8 0.9 fusion.35
  77.7 1.6 %multiply_convert_fusion.6 = bf16[256,512]{1,0:T(8,128)(2,1)S(1)} fusion(bf16[1,512,512]{2,1,0:T(8,128)(2,1)} %get-tuple-element.400, f32[512]{0:T(512)S(1)} %bitcast.71, bf16[16,128,512]{2,1,0:T(8,128)(2,1)} %get-tuple-element.399, s32[]{:T(128)S(6)} %select_n.74, bf16[16,256,128]{2,1,0:T(8,128)(2,1)} %get-tuple-element.398), kind=kOutput, calls=%fused_computation.11.clone.1 | convolution fusion | flops 168689664 | bytes 986112 | tf_op jit(solution)/shard_map/while/body/eval_jaxpr/dot_general | solution.py:9
  80.0 0.9 fusion.35
  80.8 1.6 %multiply_convert_fusion.6 = bf16[256,512]{1,0:T(8,128)(2,1)S(1)} fusion(bf16[1,512,512]{2,1,0:T(8,128)(2,1)} %get-tuple-element.400, f32[512]{0:T(512)S(1)} %bitcast.71, bf16[16,128,512]{2,1,0:T(8,128)(2,1)} %get-tuple-element.399, s32[]{:T(128)S(6)} %select_n.74, bf16[16,256,128]{2,1,0:T(8,128)(2,1)} %get-tuple-element.398), kind=kOutput, calls=%fused_computation.11.clone.1 | convolution fusion | flops 168689664 | bytes 986112 | tf_op jit(solution)/shard_map/while/body/eval_jaxpr/dot_general | solution.py:9
  82.5 0.4 fusion.34
  83.1 0.9 fusion.35
  84.0 1.6 %multiply_convert_fusion.6 = bf16[256,512]{1,0:T(8,128)(2,1)S(1)} fusion(bf16[1,512,512]{2,1,0:T(8,128)(2,1)} %get-tuple-element.400, f32[512]{0:T(512)S(1)} %bitcast.71, bf16[16,128,512]{2,1,0:T(8,128)(2,1)} %get-tuple-element.399, s32[]{:T(128)S(6)} %select_n.74, bf16[16,256,128]{2,1,0:T(8,128)(2,1)} %get-tuple-element.398), kind=kOutput, calls=%fused_computation.11.clone.1 | convolution fusion | flops 168689664 | bytes 986112 | tf_op jit(solution)/shard_map/while/body/eval_jaxpr/dot_general | solution.py:9
  85.6 0.4 fusion.34
  86.3 0.9 fusion.35
  87.1 1.6 %multiply_convert_fusion.6 = bf16[256,512]{1,0:T(8,128)(2,1)S(1)} fusion(bf16[1,512,512]{2,1,0:T(8,128)(2,1)} %get-tuple-element.400, f32[512]{0:T(512)S(1)} %bitcast.71, bf16[16,128,512]{2,1,0:T(8,128)(2,1)} %get-tuple-element.399, s32[]{:T(128)S(6)} %select_n.74, bf16[16,256,128]{2,1,0:T(8,128)(2,1)} %get-tuple-element.398), kind=kOutput, calls=%fused_computation.11.clone.1 | convolution fusion | flops 168689664 | bytes 986112 | tf_op jit(solution)/shard_map/while/body/eval_jaxpr/dot_general | solution.py:9
  88.8 0.4 fusion.34
  89.4 0.9 fusion.35
  90.3 1.6 %multiply_convert_fusion.6 = bf16[256,512]{1,0:T(8,128)(2,1)S(1)} fusion(bf16[1,512,512]{2,1,0:T(8,128)(2,1)} %get-tuple-element.400, f32[512]{0:T(512)S(1)} %bitcast.71, bf16[16,128,512]{2,1,0:T(8,128)(2,1)} %get-tuple-element.399, s32[]{:T(128)S(6)} %select_n.74, bf16[16,256,128]{2,1,0:T(8,128)(2,1)} %get-tuple-element.398), kind=kOutput, calls=%fused_computation.11.clone.1 | convolution fusion | flops 168689664 | bytes 986112 | tf_op jit(solution)/shard_map/while/body/eval_jaxpr/dot_general | solution.py:9
  91.9 0.4 fusion.34
  92.5 0.9 fusion.35
  93.4 1.6 %multiply_convert_fusion.6 = bf16[256,512]{1,0:T(8,128)(2,1)S(1)} fusion(bf16[1,512,512]{2,1,0:T(8,128)(2,1)} %get-tuple-element.400, f32[512]{0:T(512)S(1)} %bitcast.71, bf16[16,128,512]{2,1,0:T(8,128)(2,1)} %get-tuple-element.399, s32[]{:T(128)S(6)} %select_n.74, bf16[16,256,128]{2,1,0:T(8,128)(2,1)} %get-tuple-element.398), kind=kOutput, calls=%fused_computation.11.clone.1 | convolution fusion | flops 168689664 | bytes 986112 | tf_op jit(solution)/shard_map/while/body/eval_jaxpr/dot_general | solution.py:9
  95.7 0.9 fusion.35
  96.5 1.6 %multiply_convert_fusion.6 = bf16[256,512]{1,0:T(8,128)(2,1)S(1)} fusion(bf16[1,512,512]{2,1,0:T(8,128)(2,1)} %get-tuple-element.400, f32[512]{0:T(512)S(1)} %bitcast.71, bf16[16,128,512]{2,1,0:T(8,128)(2,1)} %get-tuple-element.399, s32[]{:T(128)S(6)} %select_n.74, bf16[16,256,128]{2,1,0:T(8,128)(2,1)} %get-tuple-element.398), kind=kOutput, calls=%fused_computation.11.clone.1 | convolution fusion | flops 168689664 | bytes 986112 | tf_op jit(solution)/shard_map/while/body/eval_jaxpr/dot_general | solution.py:9
  98.8 0.9 fusion.35
  99.7 1.6 %multiply_convert_fusion.6 = bf16[256,512]{1,0:T(8,128)(2,1)S(1)} fusion(bf16[1,512,512]{2,1,0:T(8,128)(2,1)} %get-tuple-element.400, f32[512]{0:T(512)S(1)} %bitcast.71, bf16[16,128,512]{2,1,0:T(8,128)(2,1)} %get-tuple-element.399, s32[]{:T(128)S(6)} %select_n.74, bf16[16,256,128]{2,1,0:T(8,128)(2,1)} %get-tuple-element.398), kind=kOutput, calls=%fused_computation.11.clone.1 | convolution fusion | flops 168689664 | bytes 986112 | tf_op jit(solution)/shard_map/while/body/eval_jaxpr/dot_general | solution.py:9
  101.9 0.9 fusion.35
  102.8 1.6 %multiply_convert_fusion.6 = bf16[256,512]{1,0:T(8,128)(2,1)S(1)} fusion(bf16[1,512,512]{2,1,0:T(8,128)(2,1)} %get-tuple-element.400, f32[512]{0:T(512)S(1)} %bitcast.71, bf16[16,128,512]{2,1,0:T(8,128)(2,1)} %get-tuple-element.399, s32[]{:T(128)S(6)} %select_n.74, bf16[16,256,128]{2,1,0:T(8,128)(2,1)} %get-tuple-element.398), kind=kOutput, calls=%fused_computation.11.clone.1 | convolution fusion | flops 168689664 | bytes 986112 | tf_op jit(solution)/shard_map/while/body/eval_jaxpr/dot_general | solution.py:9
  105.1 0.9 fusion.35
  105.9 1.6 %multiply_convert_fusion.6 = bf16[256,512]{1,0:T(8,128)(2,1)S(1)} fusion(bf16[1,512,512]{2,1,0:T(8,128)(2,1)} %get-tuple-element.400, f32[512]{0:T(512)S(1)} %bitcast.71, bf16[16,128,512]{2,1,0:T(8,128)(2,1)} %get-tuple-element.399, s32[]{:T(128)S(6)} %select_n.74, bf16[16,256,128]{2,1,0:T(8,128)(2,1)} %get-tuple-element.398), kind=kOutput, calls=%fused_computation.11.clone.1 | convolution fusion | flops 168689664 | bytes 986112 | tf_op jit(solution)/shard_map/while/body/eval_jaxpr/dot_general | solution.py:9
  108.2 0.9 fusion.35
  109.1 1.6 %multiply_convert_fusion.6 = bf16[256,512]{1,0:T(8,128)(2,1)S(1)} fusion(bf16[1,512,512]{2,1,0:T(8,128)(2,1)} %get-tuple-element.400, f32[512]{0:T(512)S(1)} %bitcast.71, bf16[16,128,512]{2,1,0:T(8,128)(2,1)} %get-tuple-element.399, s32[]{:T(128)S(6)} %select_n.74, bf16[16,256,128]{2,1,0:T(8,128)(2,1)} %get-tuple-element.398), kind=kOutput, calls=%fused_computation.11.clone.1 | convolution fusion | flops 168689664 | bytes 986112 | tf_op jit(solution)/shard_map/while/body/eval_jaxpr/dot_general | solution.py:9
  111.3 0.9 fusion.35
  112.2 1.7 %multiply_convert_fusion.6 = bf16[256,512]{1,0:T(8,128)(2,1)S(1)} fusion(bf16[1,512,512]{2,1,0:T(8,128)(2,1)} %get-tuple-element.400, f32[512]{0:T(512)S(1)} %bitcast.71, bf16[16,128,512]{2,1,0:T(8,128)(2,1)} %get-tuple-element.399, s32[]{:T(128)S(6)} %select_n.74, bf16[16,256,128]{2,1,0:T(8,128)(2,1)} %get-tuple-element.398), kind=kOutput, calls=%fused_computation.11.clone.1 | convolution fusion | flops 168689664 | bytes 986112 | tf_op jit(solution)/shard_map/while/body/eval_jaxpr/dot_general | solution.py:9
  114.5 0.9 fusion.35
  115.4 1.6 %multiply_convert_fusion.6 = bf16[256,512]{1,0:T(8,128)(2,1)S(1)} fusion(bf16[1,512,512]{2,1,0:T(8,128)(2,1)} %get-tuple-element.400, f32[512]{0:T(512)S(1)} %bitcast.71, bf16[16,128,512]{2,1,0:T(8,128)(2,1)} %get-tuple-element.399, s32[]{:T(128)S(6)} %select_n.74, bf16[16,256,128]{2,1,0:T(8,128)(2,1)} %get-tuple-element.398), kind=kOutput, calls=%fused_computation.11.clone.1 | convolution fusion | flops 168689664 | bytes 986112 | tf_op jit(solution)/shard_map/while/body/eval_jaxpr/dot_general | solution.py:9
  117.0 0.4 fusion.34
  117.6 0.9 fusion.35
  118.5 1.6 %multiply_convert_fusion.6 = bf16[256,512]{1,0:T(8,128)(2,1)S(1)} fusion(bf16[1,512,512]{2,1,0:T(8,128)(2,1)} %get-tuple-element.400, f32[512]{0:T(512)S(1)} %bitcast.71, bf16[16,128,512]{2,1,0:T(8,128)(2,1)} %get-tuple-element.399, s32[]{:T(128)S(6)} %select_n.74, bf16[16,256,128]{2,1,0:T(8,128)(2,1)} %get-tuple-element.398), kind=kOutput, calls=%fused_computation.11.clone.1 | convolution fusion | flops 168689664 | bytes 986112 | tf_op jit(solution)/shard_map/while/body/eval_jaxpr/dot_general | solution.py:9
  120.8 0.9 fusion.35
  121.6 1.6 %multiply_convert_fusion.6 = bf16[256,512]{1,0:T(8,128)(2,1)S(1)} fusion(bf16[1,512,512]{2,1,0:T(8,128)(2,1)} %get-tuple-element.400, f32[512]{0:T(512)S(1)} %bitcast.71, bf16[16,128,512]{2,1,0:T(8,128)(2,1)} %get-tuple-element.399, s32[]{:T(128)S(6)} %select_n.74, bf16[16,256,128]{2,1,0:T(8,128)(2,1)} %get-tuple-element.398), kind=kOutput, calls=%fused_computation.11.clone.1 | convolution fusion | flops 168689664 | bytes 986112 | tf_op jit(solution)/shard_map/while/body/eval_jaxpr/dot_general | solution.py:9
  123.3 0.4 fusion.34
  123.9 0.9 fusion.35
  124.8 9.4 %all_to_all.15 = f32[12,16,256]{2,0,1:T(8,128)S(1)} all-to-all(f32[12,16,256]{2,0,1:T(8,128)} %get-tuple-element.270), channel_id=1, replica_groups=mesh['band'=8,'patch'=4] {'patch'}, dimensions={1} | all-to-all | bytes 393216 | tf_op jit(solution)/shard_map/all_to_all | solution.py:67
  134.3 0.9 broadcast_in_dim_reshape.3
  (81 shorter events, 7.7 us)
Async XLA Ops:
  7.4 1.8 %copy-start = (bf16[1,2560,512]{2,1,0:T(8,128)(2,1)S(1)}, bf16[1,2560,512]{2,1,0:T(8,128)(2,1)}, u32[]{:S(2)}) copy-start(bf16[1,2560,512]{2,1,0:T(8,128)(2,1)} %param.13) | copy-start | bytes 7864324
  7.4 66.4 %all-reduce.2.cloned.1.call-start = ((), (), s32[]{:S(2)}) async-start(), calls=%async_computation.2 | async-start | bytes 4194304 | tf_op jit(solution)/shard_map/psum | solution.py:58
  9.1 9.2 %copy-start.7 = (s32[16]{0:T(128)S(1)}, s32[16]{0:T(128)}, u32[]{:S(2)}) copy-start(s32[16]{0:T(128)} %param.14) | copy-start | bytes 196
  21.2 53.3 %copy-start.1 = (bf16[1,512,512]{2,1,0:T(8,128)(2,1)S(1)}, bf16[1,512,512]{2,1,0:T(8,128)(2,1)}, u32[]{:S(2)}) copy-start(bf16[1,512,512]{2,1,0:T(8,128)(2,1)} %param.19) | copy-start | bytes 1572868
  21.2 53.3 %copy-start.2 = (bf16[1,12,512]{2,1,0:T(8,128)(2,1)S(1)}, bf16[1,12,512]{2,1,0:T(8,128)(2,1)}, u32[]{:S(2)}) copy-start(bf16[1,12,512]{2,1,0:T(8,128)(2,1)} %param.22) | copy-start | bytes 36868
  21.2 53.3 %copy-start.3 = (f32[1,512]{1,0:T(1,128)S(1)}, f32[1,512]{1,0:T(1,128)}, u32[]{:S(2)}) copy-start(f32[1,512]{1,0:T(1,128)} %param.20) | copy-start | bytes 6148
  21.2 53.3 %copy-start.4 = (f32[1,512]{1,0:T(1,128)S(1)}, f32[1,512]{1,0:T(1,128)}, u32[]{:S(2)}) copy-start(f32[1,512]{1,0:T(1,128)} %param.21) | copy-start | bytes 6148
  21.2 53.3 %copy-start.5 = (f32[1,12]{1,0:T(1,128)S(1)}, f32[1,12]{1,0:T(1,128)}, u32[]{:S(2)}) copy-start(f32[1,12]{1,0:T(1,128)} %param.23) | copy-start | bytes 148
  21.2 53.3 %copy-start.6 = (f32[1,512]{1,0:T(1,128)S(1)}, f32[1,512]{1,0:T(1,128)}, u32[]{:S(2)}) copy-start(f32[1,512]{1,0:T(1,128)} %param.18) | copy-start | bytes 6148
  21.3 52.5 %all-gather.2.cloned.1.call-start = ((), (), s32[]{:S(2)}) async-start(), calls=%async_computation.1 | async-start | bytes 1179648 | tf_op jit(solution)/shard_map/all_gather | solution.py:40
Sparse Core Ops, SparseCore 0:
  21.4 52.3 all-reduce.1
Sparse Core Ops, SparseCore 1:
  23.9 40.0 all-gather.1
where the time goes:
time: 145 us; the launch traced here: 143 us
  waiting for transfers between devices  52.5 us (36%)
  matrix products  46.4 us (32%)
  between operations  14.9 us (10%)
  local copies, waits for them, and re-layouts  11.2 us (8%)
  blocking collectives  9.38 us (6%)
  other arithmetic  7.95 us (5%)
    psum x1, waiting for transfers between devices, body(): all_blocks = lax.psum(filled.astype(jnp.bfloat16), 'patch')  51.9 us
    dot_general x16, matrix products, decode_rows(): jnp.dot(interp, w_first, preferred_element_type=jnp.float32) + b_first  26.3 us
    dot_general x16, matrix products, decode_rows(): lax.dot_general(w_out, normed, (((1,), (1,)), ((), ())), preferred_elemen...  13.9 us
    all_to_all x1, blocking collectives, body(): lax.all_to_all(decoded, 'patch', split_axis=1, concat_axis=2, tiled=True)  9.38 us
    gather x1, local copies, waits for them, and re-layouts, body(): jnp.take(local_latents, block_rows.reshape(-1), axis=0)  9.18 us
    dot_general x16, matrix products, decode_rows(): jnp.dot(hidden, w_second, preferred_element_type=jnp.float32) + b_second  6.16 us
    reduce_sum x16, other arithmetic, decode_rows(): variance = jnp.mean(centred * centred, axis=-1, keepdims=True)  3.28 us
    convert_element_type x1, other arithmetic, body(): all_blocks = lax.psum(filled.astype(jnp.bfloat16), 'patch')  2.9 us
  transfers between devices with their start and end apart: 2, of which 1 were waited for; matrix products, arithmetic and copies ran while one was open for 0% of the time, Pallas kernels for 0%

commit v1 on v0

v1 whole, which is shorter than its diff:
```python
import functools

import jax
import jax.numpy as jnp
from jax import lax
from jax.experimental import pallas as pl
from jax.experimental.pallas import tpu as pltpu
from jax.sharding import PartitionSpec as P

LEAD = 2


def kernel(
    nb, np_, tiles, blk, cl,
    owners, rows, w_b1, w_b2, w_gain, w_out, w_bo, latents, pieces, w_first, w_second,
    out,
    lat, w1, w2, perm, onehot, acc, sib, own, from_sib, from_chip, weights, block,
    lat_sem, wt_sem, piece_send, w_recv, w_send, sib_send, sib_recv, chip_send, chip_recv,
):
    b, p = lax.axis_index("band"), lax.axis_index("patch")
    n_chips = np_ // 2
    tb, tp = tiles // nb, tiles // np_
    g = tp // tb
    n_z = nb // 2
    q, c = p // 2, p % 2
    z, x = b // 2, b % 2
    units = g * tb * n_chips
    rows_u = 2 * cl
    mesh_dev, width = latents.shape
    depth = onehot.shape[1]
    mesh_type = pl.DeviceIdType.MESH

    def dev(band, patch):
        return {"band": band, "patch": patch}

    def remote(src, dst, send, recv, band, patch):
        return pltpu.make_async_remote_copy(
            src_ref=src, dst_ref=dst, send_sem=send, recv_sem=recv,
            device_id=dev(band, patch), device_id_type=mesh_type,
        )

    barrier = pltpu.get_barrier_semaphore()

    def greet(band, patch):
        pl.semaphore_signal(barrier, inc=1, device_id=dev(band, patch), device_id_type=mesh_type)

    for d in range(1, np_):
        greet(b, (p + d) % np_)
    greet(2 * z + 1 - x, p)

    @pl.when(z > 0)
    def _():
        greet(b - 2, p)

    @pl.when(z < n_z - 1)
    def _():
        greet(b + 2, p)

    lat_copies = [
        pltpu.make_async_copy(
            latents.at[pl.ds(k * depth, depth)], lat.at[pl.ds(k * depth, depth)], lat_sem.at[k]
        )
        for k in range(mesh_dev // depth)
    ]
    for copy in lat_copies:
        copy.start()
    w1_copy = pltpu.make_async_copy(w_first, w1, wt_sem.at[0])
    w2_copy = pltpu.make_async_copy(w_second, w2, wt_sem.at[1])
    w1_copy.start()
    w2_copy.start()

    offsets = list(range(1, n_chips)) + [0]
    order = []
    for d_list in (offsets[:-1], offsets[-1:]):
        for core in (1 - c, c):
            for d in d_list:
                for i in range(tp):
                    order.append((2 * ((q + d) % n_chips) + core) * tp + i)
    perm[...] = jnp.full(perm.shape, -1, jnp.int32)
    for k, t in enumerate(order):
        mine = (owners[t] == p).astype(jnp.int32)
        perm[k : k + 1, :] = rows[pl.ds(t, 1), :] * mine + (mine - 1)
    columns = perm[...].T

    pl.semaphore_wait(barrier, np_ + (z > 0).astype(jnp.int32) + (z < n_z - 1).astype(jnp.int32))

    home = b // g
    own_source = b % g
    piece_copies = [
        (
            pieces.at[i],
            weights.at[own_source * tb + i, pl.ds(pl.multiple_of(p * cl, cl), cl)],
            w_recv.at[own_source, i, q],
            piece_send.at[i],
        )
        for i in range(tb)
    ]

    @pl.when(p == home)
    def _():
        for src, dst, recv, _ in piece_copies:
            pltpu.make_async_copy(src, dst, recv).start()

    @pl.when(p != home)
    def _():
        for src, dst, recv, send in piece_copies:
            remote(src, dst, send, recv, b, home).start()

    def unit_of(n):
        jj, k = n % g, n // g
        i, dd = k // n_chips, k % n_chips
        j = (x + jj) % g
        qq = (q + dd) % n_chips
        return i, j, qq

    def chunk(n):
        i, j, qq = unit_of(n)
        return weights.at[j * tb + i, pl.ds(pl.multiple_of(qq * rows_u, rows_u), rows_u)]

    def forwards(n, act):
        i, j, qq = unit_of(n)
        source = p * g + j
        zs, xs = source // 2, source % 2
        part = chunk(n)
        recv = w_recv.at[j, i, qq]
        on_line = x == xs

        @pl.when(on_line & (z >= zs) & (z < n_z - 1))
        def _():
            act(remote(part, part, w_send.at[0, n], recv, b + 2, p))

        @pl.when(on_line & (z <= zs) & (z > 0))
        def _():
            act(remote(part, part, w_send.at[1, n], recv, b - 2, p))

        @pl.when(on_line)
        def _():
            act(remote(part, part, w_send.at[2, n], recv, 2 * z + 1 - x, p))

    def relay(n):
        i, j, qq = unit_of(n)
        part = chunk(n)
        pltpu.make_async_copy(part, part, w_recv.at[j, i, qq]).wait()
        forwards(n, lambda copy: copy.start())

    iota = lax.broadcasted_iota(jnp.int32, (blk, depth), 1)

    def gather(first, count, dst, first_time):
        for k in range(mesh_dev // depth):
            if first_time:
                lat_copies[k].wait()
            for r in range(count):
                hit = iota == (columns[:, first + r : first + r + 1] - k * depth)
                onehot[r * blk : (r + 1) * blk, :] = jnp.where(hit, 1.0, 0.0).astype(jnp.bfloat16)
            part = jnp.dot(
                onehot[: count * blk, :], lat[k * depth : (k + 1) * depth, :],
                preferred_element_type=jnp.float32,
            )
            if k:
                part = part + acc[: count * blk, :]
            if k < mesh_dev // depth - 1:
                acc[: count * blk, :] = part
            else:
                dst[...] = part.astype(jnp.bfloat16).reshape(dst.shape)

    def to_sibling(d, i):
        return remote(
            sib.at[d, i], from_sib.at[d, i], sib_send.at[d, i], sib_recv.at[d, i], b, 2 * q + 1 - c
        )

    def to_chip(d, i):
        return remote(
            own.at[d, i], from_chip.at[d - 1, i], chip_send.at[d - 1, i], chip_recv.at[d - 1, i],
            b, 2 * ((q + d) % n_chips) + c,
        )

    far = (n_chips - 1) * tp
    if n_chips > 1:
        gather(0, far, sib.at[pl.ds(1, n_chips - 1)], True)
        for d in range(1, n_chips):
            for i in range(tp):
                to_sibling(d, i).start()
        gather(far, far, own.at[pl.ds(1, n_chips - 1)], False)
        for i in range(tb):
            for jj in range(g):
                it = ((x + jj) % g) * tb + i
                for d in range(1, n_chips):
                    to_sibling(d, it).wait_recv()
                    own[d, it] = own[d, it] + from_sib[d, it]
                    to_chip(d, it).start()
    gather(2 * far, tp, sib.at[pl.ds(0, 1)], n_chips == 1)
    for i in range(tp):
        to_sibling(0, i).start()
    gather(2 * far + tp, tp, own.at[pl.ds(0, 1)], False)

    w1_copy.wait()
    w2_copy.wait()
    for n in range(min(LEAD, units)):
        relay(n)

    def decode(n, carry):
        @pl.when(n + LEAD < units)
        def _():
            relay(n + LEAD)

        i, j, qq = unit_of(n)
        tile = j * tb + i

        @pl.when((n // g) % n_chips == 0)
        def _():
            to_sibling(0, tile).wait_recv()
            total = own[0, tile] + from_sib[0, tile]
            for d in range(1, n_chips):
                to_chip(d, tile).wait_recv()
                total = total + from_chip[d - 1, tile]
            block[tile] = total

        start = pl.multiple_of(qq * rows_u, rows_u)
        interp = jnp.dot(
            weights[tile, pl.ds(start, rows_u), :], block[tile], preferred_element_type=jnp.float32
        ).astype(jnp.bfloat16)
        v = jnp.dot(interp, w1[...], preferred_element_type=jnp.float32) + w_b1[...]
        half = 0.5 * v
        hidden = (half * jnp.tanh(half) + half).astype(jnp.bfloat16)
        second = jnp.dot(hidden, w2[...], preferred_element_type=jnp.float32) + w_b2[...]
        centred = second - jnp.mean(second, axis=-1, keepdims=True)
        variance = jnp.mean(centred * centred, axis=-1, keepdims=True)
        normed = (centred * lax.rsqrt(variance + 1e-05) * w_gain[...]).astype(jnp.bfloat16)
        result = lax.dot_general(
            w_out[...], normed, (((1,), (1,)), ((), ())), preferred_element_type=jnp.float32
        )
        at = pl.multiple_of(tile * (np_ * cl) + start, rows_u)
        out[:, pl.ds(at, rows_u)] = result + w_bo[...]
        return carry

    lax.fori_loop(0, units, decode, 0)

    @pl.when(p != home)
    def _():
        for src, dst, recv, send in piece_copies:
            remote(src, dst, send, recv, b, home).wait_send()

    for d in range(n_chips):
        for i in range(tp):
            to_sibling(d, i).wait_send()
            if d:
                to_chip(d, i).wait_send()

    def drain(n, carry):
        forwards(n, lambda copy: copy.wait_send())
        return carry

    lax.fori_loop(0, units, drain, 0)


def solution(mesh):
    nb, np_ = mesh.shape["band"], mesh.shape["patch"]

    def body(
        latents, owners, block_rows, pieces, w_first, b_first, w_second, b_second, gain, w_out, b_out
    ):
        tiles, blk = block_rows.shape
        cl, channels = pieces.shape[1], w_out.shape[1]
        mesh_dev, width = latents.shape[1:]
        n_chips, tb, tp = np_ // 2, tiles // nb, tiles // np_
        g = tp // tb
        units = g * tb * n_chips
        depth = next(k for k in (512, 256, 128, mesh_dev) if mesh_dev % k == 0)
        group = max(n_chips - 1, 1) * tp * blk
        vmem = pl.BlockSpec(memory_space=pltpu.VMEM)
        hbm = pl.BlockSpec(memory_space=pl.ANY)
        bf16 = jnp.bfloat16
        dma = pltpu.SemaphoreType.DMA
        result = pl.pallas_call(
            functools.partial(kernel, nb, np_, tiles, blk, cl),
            out_shape=jax.ShapeDtypeStruct((channels, tp * np_ * cl), jnp.float32),
            in_specs=[pl.BlockSpec(memory_space=pltpu.SMEM)] + [vmem] * 6 + [hbm] * 4,
            out_specs=vmem,
            scratch_shapes=[
                pltpu.VMEM((mesh_dev, width), bf16),
                pltpu.VMEM(w_first.shape[1:], bf16),
                pltpu.VMEM(w_second.shape[1:], bf16),
                pltpu.VMEM((blk, blk), jnp.int32),
                pltpu.VMEM((group, depth), bf16),
                pltpu.VMEM((group, width), jnp.float32),
                pltpu.VMEM((n_chips, tp, blk, width), bf16),
                pltpu.VMEM((n_chips, tp, blk, width), bf16),
                pltpu.VMEM((n_chips, tp, blk, width), bf16),
                pltpu.VMEM((max(n_chips - 1, 1), tp, blk, width), bf16),
                pltpu.VMEM((tp, np_ * cl, blk), bf16),
                pltpu.VMEM((tp, blk, width), bf16),
                dma((mesh_dev // depth,)),
                dma((2,)),
                dma((tb,)),
                dma((g, tb, n_chips)),
                dma((3, units)),
                dma((n_chips, tp)),
                dma((n_chips, tp)),
                dma((max(n_chips - 1, 1), tp)),
                dma((max(n_chips - 1, 1), tp)),
            ],
            compiler_params=pltpu.CompilerParams(collective_id=0, has_side_effects=True),
            name="decode",
        )(
            owners, block_rows, b_first, b_second, gain, w_out[0], b_out.reshape(channels, 1),
            latents[0], pieces, w_first[0], w_second[0],
        )
        return result[None]

    return jax.shard_map(
        body,
        mesh=mesh,
        in_specs=(
            P("band", "patch", None),
            P(),
            P(),
            P("band", "patch", None),
            P("band", None, None),
            P("band", None),
            P("band", None, None),
            P("band", None),
            P("band", None),
            P("band", None, None),
            P("band", None),
        ),
        out_specs=P("band", None, "patch"),
        check_vma=False,
    )
```

time: 145 us -> 52 us (0.36); the launches traced: 143 us -> 51.8 us
  waiting for transfers between devices: 52.5 us -> 0 us
  Pallas kernels: 0 us -> 48.7 us
  matrix products: 46.4 us -> 0 us
  between operations: 14.9 us -> 0.01 us
  blocking collectives: 9.38 us -> 0 us
  local copies, waits for them, and re-layouts: 11.2 us -> 3.16 us
  other arithmetic: 7.95 us -> 0 us
    psum x1 -> x0, waiting for transfers between devices: 51.9 us -> none  [body(): all_blocks = lax.psum(filled.astype(jnp.bfloat16), 'patch')]
    pallas_call x0 -> x1, Pallas kernels: none -> 48.7 us  [body(): pl.pallas_call(functools.partial(kernel, nb, np_, tiles, blk, cl), out_sh...]
    dot_general x48 -> x0, matrix products: 46.4 us -> none  [the longest x16 26.3 us: decode_rows(): jnp.dot(interp, w_first, preferred_element_type=jnp.float32) + b_first]
    all_to_all x1 -> x0, blocking collectives: 9.38 us -> none  [body(): lax.all_to_all(decoded, 'patch', split_axis=1, concat_axis=2, tiled=True)]
    gather x1 -> x0, local copies, waits for them, and re-layouts: 9.18 us -> none  [body(): jnp.take(local_latents, block_rows.reshape(-1), axis=0)]
    reduce_sum x16 -> x0, other arithmetic: 3.28 us -> none  [decode_rows(): variance = jnp.mean(centred * centred, axis=-1, keepdims=True)]
    convert_element_type x1 -> x0, other arithmetic: 2.9 us -> none  [body(): all_blocks = lax.psum(filled.astype(jnp.bfloat16), 'patch')]
  transfers between devices with their start and end apart: 2 -> 0, of which waited for: 1 -> 0; matrix products, arithmetic and copies ran while one was open for 0% -> 0% of each run, Pallas kernels for 0% -> 0%
where the time goes in v1:
time: 52 us; the launch traced here: 51.8 us
  Pallas kernels  48.7 us (94%)
  local copies, waits for them, and re-layouts  3.16 us (6%)
    pallas_call x1, Pallas kernels, body(): pl.pallas_call(functools.partial(kernel, nb, np_, tiles, blk, cl), out_sh...  48.7 us
    broadcast_in_dim x1, local copies, waits for them, and re-layouts, body(): return result[None]  1.83 us
    reshape x1, local copies, waits for them, and re-layouts, body(): b_out.reshape(channels, 1)  1.33 us

profile of v1, /device:TPU:24, one launch (start us, length us, event | category | flops | bytes accessed | tf_op | source)
XLA Modules:
  0.0 51.8 jit_solution(14708505387987728890)
XLA Ops:
  0.0 1.3 %copy.12.w_bo = f32[12,1]{1,0:T(8,128)} copy(f32[12,1]{0,1:T(1,128)} %bitcast.11) | data formatting | bytes 96 | tf_op jit(solution)/shard_map/reshape | solution.py:305
  1.3 48.7 %decode.1 = f32[12,4096]{1,0:T(8,128)} custom-call(s32[16]{0:T(128)} %owners.1, s32[16,128]{1,0:T(8,128)} %rows.1, f32[1,512]{1,0:T(1,128)} %w_b1.1, f32[1,512]{1,0:T(1,128)} %w_b2.1, f32[1,512]{1,0:T(1,128)} %w_gain.1, bf16[12,512]{1,0:T(8,128)(2,1)} %bitcast.10, f32[12,1]{1,0:T(8,128)} %copy.12.w_bo, bf16[2560,512]{1,0:T(8,128)(2,1)} %bitcast.6, ...), custom_call_target="tpu_custom_call" | custom-call | tf_op jit(solution)/shard_map/decode/pallas_call | solution.py:274
  50.0 1.8 %copy.13 = f32[1,12,4096]{2,0,1:T(1,128)} copy(f32[1,12,4096]{2,1,0:T(8,128)} %bitcast.7) | data formatting | bytes 393216 | tf_op jit(solution)/shard_map/broadcast_in_dim | solution.py:308

commit v2 on v1

--- a/solution.py
+++ b/solution.py
@@ -90,7 +90,7 @@
         (
             pieces.at[i],
             weights.at[own_source * tb + i, pl.ds(pl.multiple_of(p * cl, cl), cl)],
-            w_recv.at[own_source, i, q],
+            w_recv.at[own_source, i, p],
             piece_send.at[i],
         )
         for i in range(tb)
@@ -113,35 +113,48 @@
         qq = (q + dd) % n_chips
         return i, j, qq
 
-    def chunk(n):
+    def piece(n, half):
         i, j, qq = unit_of(n)
-        return weights.at[j * tb + i, pl.ds(pl.multiple_of(qq * rows_u, rows_u), rows_u)]
-
-    def forwards(n, act):
-        i, j, qq = unit_of(n)
-        source = p * g + j
-        zs, xs = source // 2, source % 2
-        part = chunk(n)
-        recv = w_recv.at[j, i, qq]
-        on_line = x == xs
+        at = qq * 2 + half
+        part = weights.at[j * tb + i, pl.ds(pl.multiple_of(at * cl, cl), cl)]
+        return part, w_recv.at[j, i, at]
+
+    def line_of(n):
+        source = p * g + unit_of(n)[1]
+        return source // 2, x == source % 2
+
+    def forwards(n, half, act):
+        zs, on_line = line_of(n)
+        part, recv = piece(n, half)
+        slot = 2 * n + half
 
         @pl.when(on_line & (z >= zs) & (z < n_z - 1))
         def _():
-            act(remote(part, part, w_send.at[0, n], recv, b + 2, p))
+            act(remote(part, part, w_send.at[0, slot], recv, b + 2, p))
 
         @pl.when(on_line & (z <= zs) & (z > 0))
         def _():
-            act(remote(part, part, w_send.at[1, n], recv, b - 2, p))
+            act(remote(part, part, w_send.at[1, slot], recv, b - 2, p))
 
         @pl.when(on_line)
         def _():
-            act(remote(part, part, w_send.at[2, n], recv, 2 * z + 1 - x, p))
-
-    def relay(n):
-        i, j, qq = unit_of(n)
-        part = chunk(n)
-        pltpu.make_async_copy(part, part, w_recv.at[j, i, qq]).wait()
-        forwards(n, lambda copy: copy.start())
+            act(remote(part, part, w_send.at[2, slot], recv, 2 * z + 1 - x, p))
+
+    def arrive(n, half):
+        part, recv = piece(n, half)
+        pltpu.make_async_copy(part, part, recv).wait()
+
+    def relay(n, at_source):
+        zs, on_line = line_of(n)
+
+        @pl.when(on_line & ((z == zs) if at_source else (z != zs)))
+        def _():
+            for half in range(2):
+                arrive(n, half)
+                forwards(n, half, lambda copy: copy.start())
+
+    def relay_range(first, last):
+        lax.fori_loop(first, last, lambda n, carry: (relay(n, True), carry)[1], 0)
 
     iota = lax.broadcasted_iota(jnp.int32, (blk, depth), 1)
 
@@ -175,11 +188,13 @@
         )
 
     far = (n_chips - 1) * tp
+    cut = [units // 4, units // 2, units] if n_chips > 1 else [0, 0, units]
     if n_chips > 1:
         gather(0, far, sib.at[pl.ds(1, n_chips - 1)], True)
         for d in range(1, n_chips):
             for i in range(tp):
                 to_sibling(d, i).start()
+        relay_range(0, cut[0])
         gather(far, far, own.at[pl.ds(1, n_chips - 1)], False)
         for i in range(tb):
             for jj in range(g):
@@ -188,20 +203,33 @@
                     to_sibling(d, it).wait_recv()
                     own[d, it] = own[d, it] + from_sib[d, it]
                     to_chip(d, it).start()
+    relay_range(cut[0], cut[1])
     gather(2 * far, tp, sib.at[pl.ds(0, 1)], n_chips == 1)
     for i in range(tp):
         to_sibling(0, i).start()
+    relay_range(cut[1], cut[2])
     gather(2 * far + tp, tp, own.at[pl.ds(0, 1)], False)
 
     w1_copy.wait()
     w2_copy.wait()
     for n in range(min(LEAD, units)):
-        relay(n)
+        relay(n, False)
+
+    channels = w_bo.shape[1]
+    eye = lax.broadcasted_iota(jnp.int32, (channels, channels), 0) == lax.broadcasted_iota(
+        jnp.int32, (channels, channels), 1
+    )
+    bias = jnp.sum(jnp.where(eye, w_bo[...], 0.0), axis=1, keepdims=True)
 
     def decode(n, carry):
         @pl.when(n + LEAD < units)
         def _():
-            relay(n + LEAD)
+            relay(n + LEAD, False)
+
+        @pl.when(jnp.logical_not(line_of(n)[1]))
+        def _():
+            for half in range(2):
+                arrive(n, half)
 
         i, j, qq = unit_of(n)
         tile = j * tb + i
@@ -230,7 +258,9 @@
             w_out[...], normed, (((1,), (1,)), ((), ())), preferred_element_type=jnp.float32
         )
         at = pl.multiple_of(tile * (np_ * cl) + start, rows_u)
-        out[:, pl.ds(at, rows_u)] = result + w_bo[...]
+        result = result + bias
+        for ch in range(channels):
+            out[ch, :, pl.ds(at, rows_u)] = result[ch : ch + 1]
         return carry
 
     lax.fori_loop(0, units, decode, 0)
@@ -247,7 +277,8 @@
                 to_chip(d, i).wait_send()
 
     def drain(n, carry):
-        forwards(n, lambda copy: copy.wait_send())
+        for half in range(2):
+            forwards(n, half, lambda copy: copy.wait_send())
         return carry
 
     lax.fori_loop(0, units, drain, 0)
@@ -273,7 +304,7 @@
         dma = pltpu.SemaphoreType.DMA
         result = pl.pallas_call(
             functools.partial(kernel, nb, np_, tiles, blk, cl),
-            out_shape=jax.ShapeDtypeStruct((channels, tp * np_ * cl), jnp.float32),
+            out_shape=jax.ShapeDtypeStruct((channels, 1, tp * np_ * cl), jnp.float32),
             in_specs=[pl.BlockSpec(memory_space=pltpu.SMEM)] + [vmem] * 6 + [hbm] * 4,
             out_specs=vmem,
             scratch_shapes=[
@@ -292,8 +323,8 @@
                 dma((mesh_dev // depth,)),
                 dma((2,)),
                 dma((tb,)),
-                dma((g, tb, n_chips)),
-                dma((3, units)),
+                dma((g, tb, np_)),
+                dma((3, 2 * units)),
                 dma((n_chips, tp)),
                 dma((n_chips, tp)),
                 dma((max(n_chips - 1, 1), tp)),
@@ -302,10 +333,10 @@
             compiler_params=pltpu.CompilerParams(collective_id=0, has_side_effects=True),
             name="decode",
         )(
-            owners, block_rows, b_first, b_second, gain, w_out[0], b_out.reshape(channels, 1),
+            owners, block_rows, b_first, b_second, gain, w_out[0], b_out,
             latents[0], pieces, w_first[0], w_second[0],
         )
-        return result[None]
+        return jnp.transpose(result, (1, 0, 2))
 
     return jax.shard_map(
         body,

time: 52 us -> 36.5 us (0.70)
  the two profiles are of different devices: /device:TPU:24 before, /device:TPU:5 now
where the time goes in v2:
time: 36.5 us; the launch traced here: 36.3 us
  Pallas kernels  34.7 us (95%)
  local copies, waits for them, and re-layouts  1.62 us (4%)
    pallas_call x1, Pallas kernels, body(): pl.pallas_call(functools.partial(kernel, nb, np_, tiles, blk, cl), out_sh...  34.7 us
    unnamed x1, local copies, waits for them, and re-layouts  1.62 us

profile of v2, /device:TPU:5, one launch (start us, length us, event | category | flops | bytes accessed | tf_op | source)
XLA Modules:
  0.0 36.3 jit_solution(1808586068534667682)
XLA Ops:
  0.0 34.7 %decode.1 = f32[12,1,4096]{2,1,0:T(1,128)} custom-call(s32[16]{0:T(128)} %owners.1, s32[16,128]{1,0:T(8,128)} %rows.1, f32[1,512]{1,0:T(1,128)} %w_b1.1, f32[1,512]{1,0:T(1,128)} %w_b2.1, f32[1,512]{1,0:T(1,128)} %w_gain.1, bf16[12,512]{1,0:T(8,128)(2,1)} %bitcast.9, f32[1,12]{1,0:T(1,128)} %w_bo.1, bf16[2560,512]{1,0:T(8,128)(2,1)} %bitcast.5, ...), custom_call_target="tpu_custom_call" | custom-call | tf_op jit(solution)/shard_map/decode/pallas_call | solution.py:305
  34.7 1.6 %copy.13 = f32[1,12,4096]{2,0,1:T(1,128)} copy(f32[1,12,4096]{2,0,1:T(1,128)} %bitcast.6) | data formatting | bytes 393216
